TPU v7x, 32 devices: a whole 2x2x4 slice. The times are simulated.
32 devices in a mesh: patch: 16 (over z, y, core), lev: 2 (over x).
Axes of the slice: x: 2, y: 2, z: 4, core: 2. Of those that a mesh axis runs over, the one named last changes fastest.
Arguments:
- fields: float32 [3, 24, 32768], P(None, 'lev', 'patch'), may hold values from -6 to 6
- stencil_index: int32 [12, 2, 32768], P(None, 'lev', 'patch'), may hold values from 0 to 3071, as said below
- stencil_weight: float32 [12, 2, 32768], P(None, 'lev', 'patch'), may hold values from -0.2 to 0.4
- neighbours: int32 [6, 32768], P(None, 'patch'), may hold values from 0 to 2175, as said below
- lap_weight: float32 [6, 32768], P(None, 'patch'), may hold values from 0.2 to 1
- edge_x: float32 [6, 32768], P(None, 'patch'), may hold values from -1.8 to 1.8
- edge_y: float32 [6, 32768], P(None, 'patch'), may hold values from -1.8 to 1.8
- to_modes: float32 [24, 24], replicated, may hold values from -1.25 to 1.25
- from_modes: float32 [24, 24], replicated, may hold values from -1.25 to 1.25
- helm_coef: float32 [24], P('lev'), may hold values from 0.15 to 0.6
Outputs:
- new_winds: float32 [2, 24, 32768], P(None, 'lev', 'patch')
- new_height: float32 [24, 32768], P('lev', 'patch')
Inputs may be any that keep to these rules, and one draw needn't show every extreme that they name: `stencil_index`: entry [p, g, i] is a position in the cells of i's patch extended by 512 cells on each side along the closed chain; position 512 + (i mod 2048) is cell i itself, and the entry lies at most 512 from it. `neighbours`: entry [k, i] is a position in the cells of i's patch extended by 64 cells on each side along the closed chain; position 64 + (i mod 2048) is cell i itself, which is never named.
All inputs are finite; a program needn't handle non-finite values.
Results may differ from a plain program's by a relative error of at most 0.000096.
Values sent between devices are 32-bit elements; how exact they have to be, the bound alone decides.
A program may use at most 64 MiB of HBM per device.

v0:
```python
import functools
import math

import jax
import jax.numpy as jnp
from jax import lax
from jax.experimental import pallas as pl
from jax.experimental.pallas import tpu as pltpu
from jax.sharding import PartitionSpec as P

REACH = 512
NBR_REACH = 64
SWEEPS = 4
COUPLING = 0.5
LANES = 128
SUB = 8
HALO = NBR_REACH * SWEEPS
FIELD_HALO = REACH + HALO
MESH = pl.DeviceIdType.MESH


def up8(rows):
    return -(-rows // SUB) * SUB


def lanes_of(x, index):
    return jnp.take_along_axis(x, index, axis=1, mode="promise_in_bounds")


def row8(ref, row, cols):
    return jnp.broadcast_to(ref[pl.ds(row, 1), cols], (SUB, LANES))


def cols_of(block):
    return pl.ds(pl.multiple_of(block * LANES, LANES), LANES)


def loop(first, last, body, unroll=1):
    count = last - first
    while count % unroll:
        unroll -= 1

    def step(i, carry):
        for u in range(unroll):
            body(first + i * unroll + u)
        return carry

    lax.fori_loop(0, count // unroll, step, 0)


def kernel(
    npatch, nlev,
    fields_in, s_index_in, s_weight_in, nbr_in, lap_in, ex_in, ey_in, to_modes, from_modes, helm,
    winds_out, height_out,
    fields, s_index, s_weight, nbr, lap, ex, ey, winds, load_sem, wind_sem,
    f_halo, si_halo, sw_halo, nb_halo, lw_halo, ex_halo, ey_halo, hc,
    F, si, sw, nb, lw, gx, gy, U, rx, rinv, cinv, xa, xb, to_wide, from_wide,
    send_sem, recv_sem, lev_send, lev_recv, hc_send, hc_recv,
):
    group = fields.shape[1]
    cells = fields.shape[2]
    levels = group * nlev
    points = s_index.shape[0]
    sides = nbr.shape[0]
    ext = cells + 2 * HALO
    nb_blocks = ext // LANES
    hb = HALO // LANES
    patch = lax.axis_index("patch")
    lev = lax.axis_index("lev")
    right = lax.rem(patch + 1, npatch)
    left = lax.rem(patch + npatch - 1, npatch)

    barrier = pltpu.get_barrier_semaphore()
    for to in (left, right):
        pl.semaphore_signal(barrier, inc=1, device_id={"patch": to}, device_id_type=MESH)
    for d in range(1, nlev):
        pl.semaphore_signal(
            barrier, inc=1, device_id={"lev": lax.rem(lev + d, nlev)}, device_id_type=MESH
        )
    loads = []
    for no, (src, dst) in enumerate((
        (fields_in, fields), (s_index_in, s_index), (s_weight_in, s_weight),
        (nbr_in, nbr), (lap_in, lap), (ex_in, ex), (ey_in, ey),
    )):
        copy = pltpu.make_async_copy(src, dst, load_sem.at[no])
        copy.start()
        loads.append(copy)

    hc[lev] = helm[...]
    back = from_modes[0:group, :]
    for g in range(1, nlev):
        back = jnp.where(lev == g, from_modes[g * group : (g + 1) * group, :], back)
    for m in range(levels):
        to_wide[m, 0:levels] = jnp.broadcast_to(to_modes[:, m : m + 1], (levels, LANES))
        from_wide[m, 0:group] = jnp.broadcast_to(back[:, m : m + 1], (group, LANES))
    for copy in loads:
        copy.wait()
    pl.semaphore_wait(barrier, 2 + nlev - 1)

    copies = []
    pairs = (
        (fields, f_halo, FIELD_HALO),
        (s_index, si_halo, HALO),
        (s_weight, sw_halo, HALO),
        (nbr, nb_halo, HALO),
        (lap, lw_halo, HALO),
        (ex, ex_halo, HALO),
        (ey, ey_halo, HALO),
    )
    for no, (src, dst, width) in enumerate(pairs):
        lead = (slice(None),) * (len(src.shape) - 1)
        for side in (0, 1):
            start = cells - width if side == 0 else 0
            copy = pltpu.make_async_remote_copy(
                src_ref=src.at[lead + (pl.ds(start, width),)],
                dst_ref=dst.at[side],
                send_sem=send_sem.at[2 * no + side],
                recv_sem=recv_sem.at[2 * no + side],
                device_id={"patch": right if side == 0 else left},
                device_id_type=MESH,
            )
            copy.start()
            copies.append(copy)
    hc_copies = []
    for d in range(1, nlev):
        copy = pltpu.make_async_remote_copy(
            src_ref=helm,
            dst_ref=hc.at[lev],
            send_sem=hc_send.at[d - 1],
            recv_sem=hc_recv.at[d - 1],
            device_id={"lev": lax.rem(lev + d, nlev)},
            device_id_type=MESH,
        )
        copy.start()
        hc_copies.append(copy)

    for f in range(3):
        F[f * group : (f + 1) * group, FIELD_HALO : FIELD_HALO + cells] = fields[f]
    own = slice(HALO, HALO + cells)
    si[:, own] = s_index[:, 0, :] + HALO
    sw[:, own] = s_weight[:, 0, :]
    nb[:, own] = nbr[...] + (HALO - NBR_REACH)
    lw[:, own] = lap[...]
    gx[:, own] = ex[...]
    gy[:, own] = ey[...]

    frows = F.shape[0]

    def upstream(b):
        cols = cols_of(b)
        acc = [None] * (frows // SUB)
        tiles = 2 * REACH // LANES + 1
        for p in range(points):
            x = row8(si, p, cols)
            lo = x & (LANES - 1)
            hi = (x >> (LANES.bit_length() - 1)) - b
            w = row8(sw, p, cols)
            sel = [None] * (frows // SUB)
            for t in range(tiles):
                here = hi == t
                for r in range(frows // SUB):
                    taken = lanes_of(F[pl.ds(r * SUB, SUB), cols_of(b + t)], lo)
                    sel[r] = taken if t == 0 else jnp.where(here, taken, sel[r])
            for r in range(frows // SUB):
                acc[r] = w * sel[r] if acc[r] is None else acc[r] + w * sel[r]
        for r in range(frows // SUB):
            U[pl.ds(r * SUB, SUB), cols] = acc[r]

    lane = lax.broadcasted_iota(jnp.int32, (SUB, LANES), 1)
    low_half = lane < NBR_REACH

    def around(ref, b, nvregs):
        before = jnp.maximum(b - 1, 0)
        after = jnp.minimum(b + 1, nb_blocks - 1)
        own_tiles, far_tiles = [], []
        for r in range(nvregs):
            rows = pl.ds(r * SUB, SUB)
            own_tiles.append(ref[rows, cols_of(b)])
            far_tiles.append(
                jnp.where(low_half, ref[rows, cols_of(after)], ref[rows, cols_of(before)])
            )
        return own_tiles, far_tiles

    def place(k, b, cols):
        x = row8(nb, k, cols)
        return x & (LANES - 1), (x >> (LANES.bit_length() - 1)) == b

    wrows = up8(2 * group)
    sub_iota = lax.broadcasted_iota(jnp.int32, (SUB, LANES), 0)

    def right_side(b):
        cols = cols_of(b)
        nv = wrows // SUB
        own_t, far_t = around(U, b, nv)
        acc = [jnp.zeros((SUB, LANES), jnp.float32)] * nv
        for k in range(sides):
            lo, here = place(k, b, cols)
            wx, wy = row8(gx, k, cols), row8(gy, k, cols)
            for r in range(nv):
                if (r + 1) * SUB <= group:
                    w = wx
                elif r * SUB >= group:
                    w = wy
                else:
                    w = jnp.where(sub_iota + r * SUB < group, wx, wy)
                taken = jnp.where(here, lanes_of(own_t[r], lo), lanes_of(far_t[r], lo))
                acc[r] = acc[r] + w * (taken - own_t[r])
        both = jnp.concatenate(acc, axis=0)
        div = both[0:group] + both[group : 2 * group]
        rx[lev, :, cols] = U[2 * group : 3 * group, cols] - COUPLING * div

    first = hb + REACH // LANES
    last = nb_blocks - first
    chunks = ((first + 1, last - 1), (0, first + 1), (last - 1, nb_blocks))

    def send(no):
        at = pl.ds(chunks[no][0] * LANES, (chunks[no][1] - chunks[no][0]) * LANES)
        started = []
        for d in range(1, nlev):
            copy = pltpu.make_async_remote_copy(
                src_ref=rx.at[lev, :, at],
                dst_ref=rx.at[lev, :, at],
                send_sem=lev_send.at[no, d - 1],
                recv_sem=lev_recv.at[no, d - 1],
                device_id={"lev": lax.rem(lev + d, nlev)},
                device_id_type=MESH,
            )
            copy.start()
            started.append(copy)
        return started

    def arrive(side):
        for copy in copies[side::2]:
            copy.wait_recv()
        at = slice(0, FIELD_HALO) if side == 0 else slice(FIELD_HALO + cells, 2 * FIELD_HALO + cells)
        for f in range(3):
            F[f * group : (f + 1) * group, at] = f_halo[side, f]
        at = slice(0, HALO) if side == 0 else slice(HALO + cells, ext)
        shift = -cells if side == 0 else cells
        si[:, at] = si_halo[side, :, 0, :] + (HALO + shift)
        sw[:, at] = sw_halo[side, :, 0, :]
        nb[:, at] = nb_halo[side] + (HALO - NBR_REACH + shift)
        lw[:, at] = lw_halo[side]
        gx[:, at] = ex_halo[side]
        gy[:, at] = ey_halo[side]

    loop(first, last, upstream)
    loop(*chunks[0], right_side, 2)
    sends = [send(0)]
    arrive(0)
    loop(0, first, upstream)
    loop(*chunks[1], right_side, 7)
    sends.append(send(1))
    arrive(1)
    loop(last, nb_blocks, upstream)
    loop(*chunks[2], right_side, 7)
    sends.append(send(2))
    for copy in copies:
        copy.wait_send()

    for f in range(2):
        winds[:, f, :] = U[f * group : (f + 1) * group, own]
    winds_copy = pltpu.make_async_copy(winds, winds_out, wind_sem)
    winds_copy.start()

    for copy in hc_copies:
        copy.wait()
    lrows = up8(levels)
    row = lax.broadcasted_iota(jnp.int32, (lrows, group), 0)
    col = lax.broadcasted_iota(jnp.int32, (lrows, group), 1)
    c = jnp.zeros((lrows, 1), jnp.float32)
    for g in range(nlev):
        c = c + jnp.sum(jnp.where(row - g * group == col, hc[g], 0.0), axis=1, keepdims=True)
    radius = 6.0 * c / (1.0 + 6.0 * c)
    steps = [
        jnp.broadcast_to(
            1.0 / (1.0 + radius * math.cos(math.pi * (2 * j + 1) / (2.0 * SWEEPS))), (lrows, LANES)
        )
        for j in range(SWEEPS)
    ]
    c = jnp.broadcast_to(c, (lrows, LANES))

    def modal(b):
        cols = cols_of(b)
        nv = lrows // SUB
        wsum = jnp.sum(lw[:, cols], axis=0, keepdims=True)
        total = [None] * nv
        for g in range(nlev):
            for i in range(group):
                x = jnp.broadcast_to(rx[g, pl.ds(i, 1), cols], (SUB, LANES))
                for r in range(nv):
                    term = to_wide[g * group + i, pl.ds(r * SUB, SUB)] * x
                    total[r] = term if total[r] is None else total[r] + term
        for r in range(nv):
            rows = pl.ds(r * SUB, SUB)
            cr = c[r * SUB : (r + 1) * SUB]
            inv = 1.0 / (1.0 + cr * wsum)
            scaled = total[r] * inv
            rinv[rows, cols] = scaled
            cinv[rows, cols] = cr * inv
            xa[rows, cols] = steps[0][r * SUB : (r + 1) * SUB] * scaled

    for no in range(len(chunks)):
        for copy in sends[no]:
            copy.wait_recv()
        loop(*chunks[no], modal, 2)

    x_old, x_new = xa, xb
    for j in range(1, SWEEPS):
        nv = lrows // SUB

        def sweep(b, x_old=x_old, x_new=x_new, j=j):
            cols = cols_of(b)
            own_t, far_t = around(x_old, b, nv)
            acc = [None] * nv
            for k in range(sides):
                lo, here = place(k, b, cols)
                w = row8(lw, k, cols)
                for r in range(nv):
                    term = w * jnp.where(here, lanes_of(own_t[r], lo), lanes_of(far_t[r], lo))
                    acc[r] = term if acc[r] is None else acc[r] + term
            for r in range(nv):
                rows = pl.ds(r * SUB, SUB)
                s = steps[j][r * SUB : (r + 1) * SUB]
                x_new[rows, cols] = (1.0 - s) * own_t[r] + s * (
                    rinv[rows, cols] + cinv[rows, cols] * acc[r]
                )

        margin = NBR_REACH * (SWEEPS - 1 - j)
        off = hb - -(-margin // LANES)
        loop(off, nb_blocks - off, sweep, 5)
        x_old, x_new = x_new, x_old

    def heights(b):
        nv = up8(group) // SUB
        cols = cols_of(b)
        total = [None] * nv
        for m in range(levels):
            x = jnp.broadcast_to(x_old[pl.ds(m, 1), cols_of(b + hb)], (SUB, LANES))
            for r in range(nv):
                term = from_wide[m, pl.ds(r * SUB, SUB)] * x
                total[r] = term if total[r] is None else total[r] + term
        height_out[:, cols] = jnp.concatenate(total, axis=0)[0:group]

    loop(0, cells // LANES, heights, 2)
    winds_copy.wait()
    for started in sends:
        for copy in started:
            copy.wait_send()


def per_device(npatch, nlev, *args):
    fields, s_index, _, nbr = args[:4]
    _, group, cells = fields.shape
    points, sides = s_index.shape[0], nbr.shape[0]
    levels = group * nlev
    ext = cells + 2 * HALO
    f32, i32 = jnp.float32, jnp.int32
    args = args[:-1] + (args[-1].reshape(1, group),)
    lrows = up8(levels)
    vm = pltpu.VMEM
    peers = max(nlev - 1, 1)
    winds, height = pl.pallas_call(
        functools.partial(kernel, npatch, nlev),
        out_shape=(
            jax.ShapeDtypeStruct((group, 2, cells), f32),
            jax.ShapeDtypeStruct((group, cells), f32),
        ),
        in_specs=[pl.BlockSpec(memory_space=pl.ANY)] * 7
        + [pl.BlockSpec(memory_space=pltpu.VMEM)] * 3,
        out_specs=(
            pl.BlockSpec(memory_space=pl.ANY),
            pl.BlockSpec(memory_space=pltpu.VMEM),
        ),
        scratch_shapes=[vm(a.shape, a.dtype) for a in args[:7]]
        + [
            vm((group, 2, cells), f32),
            pltpu.SemaphoreType.DMA((7,)),
            pltpu.SemaphoreType.DMA,
            vm((2, 3, group, FIELD_HALO), f32),
            vm((2, points, 1, HALO), i32),
            vm((2, points, 1, HALO), f32),
            vm((2, sides, HALO), i32),
            vm((2, sides, HALO), f32),
            vm((2, sides, HALO), f32),
            vm((2, sides, HALO), f32),
            vm((nlev, 1, group), f32),
            vm((up8(3 * group), cells + 2 * FIELD_HALO), f32),
            vm((points, ext), i32),
            vm((points, ext), f32),
            vm((sides, ext), i32),
            vm((sides, ext), f32),
            vm((sides, ext), f32),
            vm((sides, ext), f32),
            vm((up8(3 * group), ext), f32),
            vm((nlev, group, ext), f32),
            vm((lrows, ext), f32),
            vm((lrows, ext), f32),
            vm((lrows, ext), f32),
            vm((lrows, ext), f32),
            vm((levels, lrows, LANES), f32),
            vm((levels, up8(group), LANES), f32),
            pltpu.SemaphoreType.DMA((14,)),
            pltpu.SemaphoreType.DMA((14,)),
            pltpu.SemaphoreType.DMA((3, peers)),
            pltpu.SemaphoreType.DMA((3, peers)),
            pltpu.SemaphoreType.DMA((peers,)),
            pltpu.SemaphoreType.DMA((peers,)),
        ],
        compiler_params=pltpu.CompilerParams(
            collective_id=0, has_side_effects=True
        ),
    )(*args)
    return jnp.transpose(winds, (1, 0, 2)), height


def solution(mesh):
    in_specs = (
        P(None, "lev", "patch"),
        P(None, "lev", "patch"),
        P(None, "lev", "patch"),
        P(None, "patch"),
        P(None, "patch"),
        P(None, "patch"),
        P(None, "patch"),
        P(),
        P(),
        P("lev"),
    )
    out_specs = (P(None, "lev", "patch"), P("lev", "patch"))
    body = functools.partial(per_device, mesh.shape["patch"], mesh.shape["lev"])
    return jax.shard_map(
        body, mesh=mesh, in_specs=in_specs, out_specs=out_specs, check_vma=False
    )
```

profile of v0, /device:TPU:0, one launch (start us, length us, event | category | flops | bytes accessed | tf_op | source)
XLA Modules:
  0.0 33.9 jit_solution(12542354242172520953)
XLA Ops:
  0.6 30.9 %shard_map.113 = (f32[12,2,2048]{2,1,0:T(2,128)}, f32[12,2048]{1,0:T(8,128)}) custom-call(f32[3,12,2048]{2,1,0:T(8,128)} %fields_in.1, s32[12,1,2048]{2,1,0:T(1,128)} %s_index_in.1, f32[12,1,2048]{2,1,0:T(1,128)} %s_weight_in.1, s32[6,2048]{1,0:T(8,128)} %nbr_in.1, f32[6,2048]{1,0:T(8,128)} %lap_in.1, f32[6,2048]{1,0:T(8,128)} %ex_in.1, f32[6,2048]{1,0:T(8,128)} %ey_in.1, ...), custom_call_target="tpu_custom_call" | custom-call | tf_op jit(solution)/shard_map/pallas_call | solution.py:363
  31.6 0.0 copy-start
  31.6 1.7 %copy.14 = f32[2,12,2048]{2,0,1:T(2,128)} copy(f32[2,12,2048]{2,0,1:T(2,128)} %bitcast.2) | data formatting | bytes 393216
  33.2 0.0 copy-done
  33.2 0.7 %copy.15 = f32[12,2048]{1,0:T(8,128)} copy(f32[12,2048]{1,0:T(8,128)S(1)} %copy-done) | data formatting | bytes 196608
Async XLA Ops:
  31.6 1.7 %copy-start = (f32[12,2048]{1,0:T(8,128)S(1)}, f32[12,2048]{1,0:T(8,128)}, u32[]{:S(2)}) copy-start(f32[12,2048]{1,0:T(8,128)} %get-tuple-element.9) | copy-start | bytes 294916
where the time goes:
time: 34.1 us; the launch traced here: 33.9 us
  Pallas kernels  30.9 us (91%)
  local copies, waits for them, and re-layouts  2.31 us (7%)
  between operations  0.65 us (2%)
    pallas_call x1, Pallas kernels, per_device(): pl.pallas_call(functools.partial(kernel, npatch, nlev), out_shape=(jax.Sh...  30.9 us
    unnamed x4, local copies, waits for them, and re-layouts  2.31 us

commit v1 on v0

--- a/solution.py
+++ b/solution.py
@@ -54,7 +54,7 @@
     winds_out, height_out,
     fields, s_index, s_weight, nbr, lap, ex, ey, winds, load_sem, wind_sem,
     f_halo, si_halo, sw_halo, nb_halo, lw_halo, ex_halo, ey_halo, hc,
-    F, si, sw, nb, lw, gx, gy, U, rx, rinv, cinv, xa, xb, to_wide, from_wide,
+    F, G0, G1, si, sw, nb, lw, gx, gy, U, rx, rinv, cinv, xa, xb, to_wide, from_wide,
     send_sem, recv_sem, lev_send, lev_recv, hc_send, hc_recv,
 ):
     group = fields.shape[1]
@@ -145,26 +145,76 @@
     gy[:, own] = ey[...]
 
     frows = F.shape[0]
-
-    def upstream(b):
+    tiles = 2 * REACH // LANES + 1
+    ftiles = F.shape[1] // LANES
+    own_lo = FIELD_HALO // LANES
+    own_hi = own_lo + cells // LANES
+
+    def split_tiles(first_tile, last_tile, to):
+        base = first_tile * frows + (frows if first_tile % 2 else 0) % (2 * SUB)
+        rows = 2 * frows
+        for no, tile in enumerate(range(first_tile, last_tile, 2)):
+            pair = [
+                F[:, min(t, ftiles - 1) * LANES : (min(t, ftiles - 1) + 1) * LANES]
+                for t in (tile, tile + 1)
+            ]
+            x = jnp.concatenate(pair, axis=0)
+            high = x.astype(jnp.bfloat16)
+            at = slice(base + no * rows, base + (no + 1) * rows)
+            to[at, 0:LANES] = high
+            to[at, LANES : 2 * LANES] = (x - high.astype(jnp.float32)).astype(jnp.bfloat16)
+
+    split_tiles(own_lo, own_hi, G0)
+    split_tiles(own_lo + 1, own_hi, G1)
+    lane_id = lax.broadcasted_iota(jnp.int32, (LANES, LANES), 0).astype(jnp.float32).astype(jnp.bfloat16)
+    one = jnp.ones((LANES, LANES), jnp.bfloat16)
+    zero = jnp.zeros((LANES, LANES), jnp.bfloat16)
+
+    by_product = points - 2 * (points // 6)
+
+    def upstream(b, odd):
         cols = cols_of(b)
         acc = [None] * (frows // SUB)
-        tiles = 2 * REACH // LANES + 1
-        for p in range(points):
-            x = row8(si, p, cols)
-            lo = x & (LANES - 1)
-            hi = (x >> (LANES.bit_length() - 1)) - b
-            w = row8(sw, p, cols)
-            sel = [None] * (frows // SUB)
-            for t in range(tiles):
-                here = hi == t
+        start = pl.multiple_of(b * frows + (frows if odd else 0) % (2 * SUB), 2 * SUB)
+        field = (G1 if odd else G0)[pl.ds(start, tiles * frows), :]
+        for p in range(0, points, 2):
+            pair = (p, p + 1)
+            his, los = [], []
+            for q in pair:
+                x = row8(si, q, cols)
+                his.append((x >> (LANES.bit_length() - 1)) - b)
+                los.append(x & (LANES - 1))
+            if p < by_product:
+                hot = []
+                for lo in los:
+                    lo = jnp.broadcast_to(lo[0:1].astype(jnp.float32), (LANES, LANES))
+                    h = jnp.where(lane_id == lo.astype(jnp.bfloat16), one, zero)
+                    hot.append(jnp.concatenate([h, h], axis=0))
+                got = jnp.dot(
+                    field, jnp.concatenate(hot, axis=1), preferred_element_type=jnp.float32
+                )
+            for no, q in enumerate(pair):
+                w = row8(sw, q, cols)
+                here = [his[no] == t for t in range(tiles)]
                 for r in range(frows // SUB):
-                    taken = lanes_of(F[pl.ds(r * SUB, SUB), cols_of(b + t)], lo)
-                    sel[r] = taken if t == 0 else jnp.where(here, taken, sel[r])
-            for r in range(frows // SUB):
-                acc[r] = w * sel[r] if acc[r] is None else acc[r] + w * sel[r]
+                    sel = None
+                    for t in range(tiles):
+                        at = t * frows + r * SUB
+                        if p < by_product:
+                            taken = got[at : at + SUB, no * LANES : (no + 1) * LANES]
+                        else:
+                            taken = lanes_of(F[pl.ds(r * SUB, SUB), cols_of(b + t)], los[no])
+                        sel = taken if t == 0 else jnp.where(here[t], taken, sel)
+                    acc[r] = w * sel if acc[r] is None else acc[r] + w * sel
         for r in range(frows // SUB):
             U[pl.ds(r * SUB, SUB), cols] = acc[r]
+
+    def upstreams(first, last):
+        def both(i):
+            upstream(first + 2 * i, False)
+            upstream(first + 2 * i + 1, True)
+
+        loop(0, (last - first) // 2, both)
 
     lane = lax.broadcasted_iota(jnp.int32, (SUB, LANES), 1)
     low_half = lane < NBR_REACH
@@ -244,15 +294,19 @@
         gx[:, at] = ex_halo[side]
         gy[:, at] = ey_halo[side]
 
-    loop(first, last, upstream)
+    upstreams(first, last)
     loop(*chunks[0], right_side, 2)
     sends = [send(0)]
     arrive(0)
-    loop(0, first, upstream)
+    split_tiles(0, own_lo, G0)
+    split_tiles(1, own_lo + 1, G1)
+    upstreams(0, first)
     loop(*chunks[1], right_side, 7)
     sends.append(send(1))
     arrive(1)
-    loop(last, nb_blocks, upstream)
+    split_tiles(own_hi, ftiles, G0)
+    split_tiles(own_hi - 1, ftiles, G1)
+    upstreams(last, nb_blocks)
     loop(*chunks[2], right_side, 7)
     sends.append(send(2))
     for copy in copies:
@@ -386,6 +440,8 @@
             vm((2, sides, HALO), f32),
             vm((nlev, 1, group), f32),
             vm((up8(3 * group), cells + 2 * FIELD_HALO), f32),
+            vm((up8(3 * group) * ((cells + 2 * FIELD_HALO) // LANES + 2), 2 * LANES), jnp.bfloat16),
+            vm((up8(3 * group) * ((cells + 2 * FIELD_HALO) // LANES + 2), 2 * LANES), jnp.bfloat16),
             vm((points, ext), i32),
             vm((points, ext), f32),
             vm((sides, ext), i32),

time: 34.1 us -> 28.2 us (0.83)
  Pallas kernels: 30.9 us -> 25 us
    pallas_call x1, Pallas kernels: 30.9 us -> 25 us  [per_device(): pl.pallas_call(functools.partial(kernel, npatch, nlev), out_shape=(jax.Sh...]
where the time goes in v1:
time: 28.2 us; the launch traced here: 28 us
  Pallas kernels  25 us (89%)
  local copies, waits for them, and re-layouts  2.31 us (8%)
  between operations  0.65 us (2%)
    pallas_call x1, Pallas kernels, per_device(): pl.pallas_call(functools.partial(kernel, npatch, nlev), out_shape=(jax.Sh...  25 us
    unnamed x4, local copies, waits for them, and re-layouts  2.31 us

profile of v1, /device:TPU:0, one launch (start us, length us, event | category | flops | bytes accessed | tf_op | source)
XLA Modules:
  0.0 28.0 jit_solution(10743896481467250738)
XLA Ops:
  0.6 25.0 %shard_map.113 = (f32[12,2,2048]{2,1,0:T(2,128)}, f32[12,2048]{1,0:T(8,128)}) custom-call(f32[3,12,2048]{2,1,0:T(8,128)} %fields_in.1, s32[12,1,2048]{2,1,0:T(1,128)} %s_index_in.1, f32[12,1,2048]{2,1,0:T(1,128)} %s_weight_in.1, s32[6,2048]{1,0:T(8,128)} %nbr_in.1, f32[6,2048]{1,0:T(8,128)} %lap_in.1, f32[6,2048]{1,0:T(8,128)} %ex_in.1, f32[6,2048]{1,0:T(8,128)} %ey_in.1, ...), custom_call_target="tpu_custom_call" | custom-call | tf_op jit(solution)/shard_map/pallas_call | solution.py:417
  25.6 0.0 copy-start
  25.6 1.7 %copy.14 = f32[2,12,2048]{2,0,1:T(2,128)} copy(f32[2,12,2048]{2,0,1:T(2,128)} %bitcast.2) | data formatting | bytes 393216
  27.3 0.0 copy-done
  27.3 0.7 %copy.15 = f32[12,2048]{1,0:T(8,128)} copy(f32[12,2048]{1,0:T(8,128)S(1)} %copy-done) | data formatting | bytes 196608
Async XLA Ops:
  25.6 1.7 %copy-start = (f32[12,2048]{1,0:T(8,128)S(1)}, f32[12,2048]{1,0:T(8,128)}, u32[]{:S(2)}) copy-start(f32[12,2048]{1,0:T(8,128)} %get-tuple-element.9) | copy-start | bytes 294916

commit v2 on v0

v2 whole, which is shorter than its diff:
```python
import functools
import math

import jax
import jax.numpy as jnp
from jax import lax
from jax.experimental import pallas as pl
from jax.experimental.pallas import tpu as pltpu
from jax.sharding import PartitionSpec as P

REACH = 512
NBR_REACH = 64
SWEEPS = 4
COUPLING = 0.5
LANES = 128
SUB = 8
HALO = NBR_REACH * SWEEPS
FIELD_HALO = REACH + HALO
MESH = pl.DeviceIdType.MESH


BITS = LANES.bit_length() - 1
bf16, f32, i32 = jnp.bfloat16, jnp.float32, jnp.int32


def up8(rows):
    return -(-rows // SUB) * SUB


def split(x):
    high = x.astype(bf16)
    return high, (x - high.astype(f32)).astype(bf16)


def product(parts, x):
    high, low = split(x)
    dot = functools.partial(jnp.dot, preferred_element_type=f32)
    return dot(parts[0], high) + (dot(parts[1], high) + dot(parts[0], low))


def lanes_of(x, index):
    return jnp.take_along_axis(x, index, axis=1, mode="promise_in_bounds")


def row8(ref, row, cols):
    return jnp.broadcast_to(ref[pl.ds(row, 1), cols], (SUB, LANES))


def cols_of(block):
    if isinstance(block, int):
        return slice(block * LANES, (block + 1) * LANES)
    return pl.ds(pl.multiple_of(block * LANES, LANES), LANES)


def loop(first, count, body, unroll=1):
    trips = count // unroll

    def step(i, carry):
        for u in range(unroll):
            body(first + i * unroll + u)
        return carry

    if trips == 1:
        step(0, 0)
    else:
        lax.fori_loop(0, trips, step, 0)
    for u in range(trips * unroll, count):
        body(first + u)


def kernel(
    npatch, nlev,
    fields_in, s_index_in, s_weight_in, nbr_in, lap_in, ex_in, ey_in, to_modes, from_modes, helm,
    winds_out, height_out,
    fields, s_index, s_weight, nbr, lap, ex, ey, winds, load_sem, wind_sem,
    f_halo, si_halo, sw_halo, nb_halo, lw_halo, ex_halo, ey_halo, hc,
    F, G0, G1, si, sw, nb, lw, gx, gy, U, rx, rinv, cinv, xa, xb,
    send_sem, recv_sem, lev_send, lev_recv, hc_send, hc_recv,
):
    group = fields.shape[1]
    cells = fields.shape[2]
    levels = group * nlev
    points = s_index.shape[0]
    sides = nbr.shape[0]
    ext = cells + 2 * HALO
    nb_blocks = ext // LANES
    own_blocks = cells // LANES
    hb = HALO // LANES
    patch = lax.axis_index("patch")
    lev = lax.axis_index("lev")
    right = lax.rem(patch + 1, npatch)
    left = lax.rem(patch + npatch - 1, npatch)

    barrier = pltpu.get_barrier_semaphore()
    for to in (left, right):
        pl.semaphore_signal(barrier, inc=1, device_id={"patch": to}, device_id_type=MESH)
    for d in range(1, nlev):
        pl.semaphore_signal(
            barrier, inc=1, device_id={"lev": lax.rem(lev + d, nlev)}, device_id_type=MESH
        )
    loads = []
    for no, (src, dst) in enumerate((
        (fields_in, fields), (s_index_in, s_index), (s_weight_in, s_weight),
        (nbr_in, nbr), (lap_in, lap), (ex_in, ex), (ey_in, ey),
    )):
        copy = pltpu.make_async_copy(src, dst, load_sem.at[no])
        copy.start()
        loads.append(copy)
    hc[lev] = helm[...]

    pairs = (
        (s_index_in, si_halo, HALO),
        (s_weight_in, sw_halo, HALO),
        (fields_in, f_halo, FIELD_HALO),
        (nbr_in, nb_halo, HALO),
        (ex_in, ex_halo, HALO),
        (ey_in, ey_halo, HALO),
        (lap_in, lw_halo, HALO),
    )

    def halo_copies(side):
        made = []
        for no, (src, dst, width) in enumerate(pairs):
            lead = (slice(None),) * (len(src.shape) - 1)
            start = (1 - side) * (cells - width)
            if not isinstance(side, int):
                start = pl.multiple_of(start, LANES)
            made.append(pltpu.make_async_remote_copy(
                src_ref=src.at[lead + (pl.ds(start, width),)],
                dst_ref=dst.at[side],
                send_sem=send_sem.at[2 * no + side],
                recv_sem=recv_sem.at[2 * no + side],
                device_id={"patch": lax.rem(patch + npatch + 1 - 2 * side, npatch)},
                device_id_type=MESH,
            ))
        return made

    def helm_copies():
        return [
            pltpu.make_async_remote_copy(
                src_ref=helm,
                dst_ref=hc.at[lev],
                send_sem=hc_send.at[d - 1],
                recv_sem=hc_recv.at[d - 1],
                device_id={"lev": lax.rem(lev + d, nlev)},
                device_id_type=MESH,
            )
            for d in range(1, nlev)
        ]

    def meet_and_send():
        pl.semaphore_wait(barrier, 2 + nlev - 1)
        for side in (0, 1):
            for copy in halo_copies(side):
                copy.start()
        for copy in helm_copies():
            copy.start()

    @pl.when(patch != 0)
    def _():
        meet_and_send()

    frows = F.shape[0]
    tiles = 2 * REACH // LANES + 1
    ftiles = F.shape[1] // LANES
    own_lo = FIELD_HALO // LANES
    own_hi = own_lo + own_blocks

    def split_pair(tile, odd, to):
        start = tile * frows + (frows if odd else 0) % (2 * SUB)
        if not isinstance(tile, int):
            start = pl.multiple_of(start, 2 * SUB)
        rows = pl.ds(start, 2 * frows)
        high, low = split(
            jnp.concatenate([F[:, cols_of(tile)], F[:, cols_of(tile + 1)]], axis=0)
        )
        to[rows, 0:LANES] = high
        to[rows, LANES : 2 * LANES] = low

    lane_id = lax.broadcasted_iota(i32, (LANES, LANES), 0).astype(f32).astype(bf16)
    one = jnp.ones((LANES, LANES), bf16)
    zero = jnp.zeros((LANES, LANES), bf16)

    def upstream(b, odd, by_lane=(2, 5)):
        cols = cols_of(b)
        nv = frows // SUB
        acc = [None] * nv
        start = b * frows + (frows if odd else 0) % (2 * SUB)
        if not isinstance(b, int):
            start = pl.multiple_of(start, 2 * SUB)
        field = (G1 if odd else G0).at[pl.ds(start, tiles * frows), :]
        for pair_no in range(points // 2):
            pair = (2 * pair_no, 2 * pair_no + 1)
            his, los = [], []
            for q in pair:
                x = row8(si, q, cols)
                his.append((x >> BITS) - b)
                los.append(x & (LANES - 1))
            on_lanes = pair_no in by_lane
            if not on_lanes:
                hot = []
                for lo in los:
                    lo = jnp.broadcast_to(lo[0:1].astype(f32), (LANES, LANES))
                    h = jnp.where(lane_id == lo.astype(bf16), one, zero)
                    hot.append(jnp.concatenate([h, h], axis=0))
                got = jnp.dot(
                    field[...], jnp.concatenate(hot, axis=1), preferred_element_type=f32
                )
            for no, q in enumerate(pair):
                w = row8(sw, q, cols)
                here = [his[no] == t for t in range(tiles)]
                for r in range(nv):
                    sel = None
                    for t in range(tiles):
                        row = t * frows + r * SUB
                        if on_lanes:
                            taken = lanes_of(
                                F[r * SUB : (r + 1) * SUB, cols_of(b + t)], los[no]
                            )
                        else:
                            taken = got[row : row + SUB, no * LANES : (no + 1) * LANES]
                        sel = taken if sel is None else jnp.where(here[t], taken, sel)
                    acc[r] = w * sel if acc[r] is None else acc[r] + w * sel
        for r in range(nv):
            U[r * SUB : (r + 1) * SUB, cols] = acc[r]

    lane = lax.broadcasted_iota(i32, (SUB, LANES), 1)
    low_half = lane < NBR_REACH

    def around(ref, b, nvregs):
        before = jnp.maximum(b - 1, 0)
        after = jnp.minimum(b + 1, nb_blocks - 1)
        own_tiles, far_tiles = [], []
        for r in range(nvregs):
            rows = pl.ds(r * SUB, SUB)
            own_tiles.append(ref[rows, cols_of(b)])
            far_tiles.append(
                jnp.where(low_half, ref[rows, cols_of(after)], ref[rows, cols_of(before)])
            )
        return own_tiles, far_tiles

    def place(k, b, cols):
        x = row8(nb, k, cols)
        return x & (LANES - 1), (x >> BITS) == b

    wrows = up8(2 * group)
    sub_iota = lax.broadcasted_iota(i32, (SUB, LANES), 0)

    def right_side(b):
        cols = cols_of(b)
        nv = wrows // SUB
        own_t, far_t = around(U, b, nv)
        acc = [jnp.zeros((SUB, LANES), f32)] * nv
        for k in range(sides):
            lo, here = place(k, b, cols)
            wx, wy = row8(gx, k, cols), row8(gy, k, cols)
            for r in range(nv):
                if (r + 1) * SUB <= group:
                    w = wx
                elif r * SUB >= group:
                    w = wy
                else:
                    w = jnp.where(sub_iota + r * SUB < group, wx, wy)
                taken = jnp.where(here, lanes_of(own_t[r], lo), lanes_of(far_t[r], lo))
                acc[r] = acc[r] + w * (taken - own_t[r])
        both = jnp.concatenate(acc, axis=0)
        div = both[0:group] + both[group : 2 * group]
        rx[lev, :, cols] = U[2 * group : 3 * group, cols] - COUPLING * div

    first = hb + REACH // LANES
    last = nb_blocks - first
    inner = (first + 1, last - first - 2)
    outer = first + 1

    def lev_copies(no, at, count):
        at = pl.ds(at * LANES if isinstance(at, int) else pl.multiple_of(at * LANES, LANES), count * LANES)
        return [
            pltpu.make_async_remote_copy(
                src_ref=rx.at[lev, :, at],
                dst_ref=rx.at[lev, :, at],
                send_sem=lev_send.at[no, d - 1],
                recv_sem=lev_recv.at[no, d - 1],
                device_id={"lev": lax.rem(lev + d, nlev)},
                device_id_type=MESH,
            )
            for d in range(1, nlev)
        ]

    def arrive(side):
        for copy in halo_copies(side):
            copy.wait_recv()
        at = pl.ds(pl.multiple_of(side * (FIELD_HALO + cells), LANES), FIELD_HALO)
        for f in range(3):
            F[f * group : (f + 1) * group, at] = f_halo[side, f]
        for i in range(0, own_lo, 2):
            split_pair(side * own_hi + i, False, G0)
        for i in range(1, own_lo + 2, 2):
            split_pair(side * (own_hi - 2) + i, True, G1)
        at = pl.ds(pl.multiple_of(side * (HALO + cells), LANES), HALO)
        shift = HALO + (2 * side - 1) * cells
        si[:, at] = si_halo[side, :, 0, :] + shift
        sw[:, at] = sw_halo[side, :, 0, :]
        nb[:, at] = nb_halo[side] + (shift - NBR_REACH)
        lw[:, at] = lw_halo[side]
        gx[:, at] = ex_halo[side]
        gy[:, at] = ey_halo[side]

    for copy in loads:
        copy.wait()
    for f in range(3):
        F[f * group : (f + 1) * group, FIELD_HALO : FIELD_HALO + cells] = fields[f]
    own = slice(HALO, HALO + cells)
    si[:, own] = s_index[:, 0, :] + HALO
    sw[:, own] = s_weight[:, 0, :]
    for tile in range(own_lo, own_hi, 2):
        split_pair(tile, False, G0)
    for tile in range(own_lo + 1, own_hi, 2):
        split_pair(tile, True, G1)
    for b in range(first, last):
        upstream(b, b % 2)
    nb[:, own] = nbr[...] + (HALO - NBR_REACH)
    lw[:, own] = lap[...]
    gx[:, own] = ex[...]
    gy[:, own] = ey[...]

    @pl.when(patch == 0)
    def _():
        meet_and_send()

    loop(*inner, right_side, inner[1])
    for copy in lev_copies(0, *inner):
        copy.start()
    begin = jnp.where(patch == 1, 1, 1 - lax.rem(patch, 2))

    def flank(turn, carry):
        side = begin + turn * (1 - 2 * begin)
        arrive(side)
        for i in range(first):
            upstream(side * last + i, i % 2)
        loop(side * (last - 1), outer, right_side, outer)
        for copy in lev_copies(1 + turn, side * (last - 1), outer):
            copy.start()
        return carry

    lax.fori_loop(0, 2, flank, 0)

    for f in range(2):
        winds[:, f, :] = U[f * group : (f + 1) * group, own]
    winds_copy = pltpu.make_async_copy(winds, winds_out, wind_sem)
    winds_copy.start()

    for copy in helm_copies():
        copy.wait()
    lrows = up8(levels)
    row = lax.broadcasted_iota(i32, (lrows, group), 0)
    col = lax.broadcasted_iota(i32, (lrows, group), 1)
    c = jnp.zeros((lrows, 1), f32)
    for g in range(nlev):
        c = c + jnp.sum(jnp.where(row - g * group == col, hc[g], 0.0), axis=1, keepdims=True)
    radius = 6.0 * c / (1.0 + 6.0 * c)
    steps = [
        jnp.broadcast_to(
            1.0 / (1.0 + radius * math.cos(math.pi * (2 * j + 1) / (2.0 * SWEEPS))), (lrows, LANES)
        )
        for j in range(SWEEPS)
    ]
    c = jnp.broadcast_to(c, (lrows, LANES))
    nv = lrows // SUB
    to_parts = split(to_modes[...])
    back = from_modes[0:group, :]
    for g in range(1, nlev):
        back = jnp.where(lev == g, from_modes[g * group : (g + 1) * group, :], back)
    back_parts = split(back)

    def modal(b):
        cols = cols_of(b)
        wsum = jnp.sum(lw[:, cols], axis=0, keepdims=True)
        total = product(to_parts, jnp.concatenate([rx[g, :, cols] for g in range(nlev)], axis=0))
        for r in range(nv):
            rows = pl.ds(r * SUB, SUB)
            cr = c[r * SUB : (r + 1) * SUB]
            inv = 1.0 / (1.0 + cr * wsum)
            scaled = total[r * SUB : (r + 1) * SUB] * inv
            rinv[rows, cols] = scaled
            cinv[rows, cols] = cr * inv
            xa[rows, cols] = steps[0][r * SUB : (r + 1) * SUB] * scaled

    def sweep(j, b):
        x_old, x_new = (xa, xb) if j % 2 else (xb, xa)
        cols = cols_of(b)
        own_t, far_t = around(x_old, b, nv)
        acc = [None] * nv
        for k in range(sides):
            lo, here = place(k, b, cols)
            w = row8(lw, k, cols)
            for r in range(nv):
                term = w * jnp.where(here, lanes_of(own_t[r], lo), lanes_of(far_t[r], lo))
                acc[r] = term if acc[r] is None else acc[r] + term
        for r in range(nv):
            rows = pl.ds(r * SUB, SUB)
            s = steps[j][r * SUB : (r + 1) * SUB]
            x_new[rows, cols] = (1.0 - s) * own_t[r] + s * (
                rinv[rows, cols] + cinv[rows, cols] * acc[r]
            )

    x_end = xa if SWEEPS % 2 else xb

    def heights(b):
        height_out[:, cols_of(b - hb)] = product(back_parts, x_end[0:levels, cols_of(b)])

    def off(j):
        return hb - -(-(NBR_REACH * (SWEEPS - 1 - j)) // LANES)

    def finish(side, first_part):
        def part(at, j):
            width = nb_blocks - outer if first_part else outer
            low = (nb_blocks - width) * side
            if j == 0:
                return low, width
            grow = -j if first_part else j
            width = width + grow - at
            return low + jnp.where(side == 0, at, -grow), width

        many = 1 if nv > 4 else nb_blocks
        loop(*part(0, 0), modal, min(many, part(0, 0)[1]))
        for j in range(1, SWEEPS):
            start, count = part(off(j), j)
            loop(start, count, functools.partial(sweep, j), min(many, count))
        start, count = part(hb, SWEEPS - 1)
        loop(start, count, heights, count)

    for copy in lev_copies(0, *inner) + lev_copies(1, begin * (last - 1), outer):
        copy.wait_recv()
    finish(begin, True)
    for copy in lev_copies(2, (1 - begin) * (last - 1), outer):
        copy.wait_recv()
    finish(1 - begin, False)
    winds_copy.wait()
    for side in (0, 1):
        for copy in halo_copies(side):
            copy.wait_send()
    for copy in lev_copies(0, *inner):
        copy.wait_send()
    for no in (1, 2):
        for copy in lev_copies(no, 0, outer):
            copy.wait_send()


def per_device(npatch, nlev, *args):
    fields, s_index, _, nbr = args[:4]
    _, group, cells = fields.shape
    points, sides = s_index.shape[0], nbr.shape[0]
    levels = group * nlev
    ext = cells + 2 * HALO
    args = args[:-1] + (args[-1].reshape(1, group),)
    lrows = up8(levels)
    vm = pltpu.VMEM
    peers = max(nlev - 1, 1)
    winds, height = pl.pallas_call(
        functools.partial(kernel, npatch, nlev),
        out_shape=(
            jax.ShapeDtypeStruct((group, 2, cells), f32),
            jax.ShapeDtypeStruct((group, cells), f32),
        ),
        in_specs=[pl.BlockSpec(memory_space=pl.ANY)] * 7
        + [pl.BlockSpec(memory_space=pltpu.VMEM)] * 3,
        out_specs=(
            pl.BlockSpec(memory_space=pl.ANY),
            pl.BlockSpec(memory_space=pltpu.VMEM),
        ),
        scratch_shapes=[vm(a.shape, a.dtype) for a in args[:7]]
        + [
            vm((group, 2, cells), f32),
            pltpu.SemaphoreType.DMA((7,)),
            pltpu.SemaphoreType.DMA,
            vm((2, 3, group, FIELD_HALO), f32),
            vm((2, points, 1, HALO), i32),
            vm((2, points, 1, HALO), f32),
            vm((2, sides, HALO), i32),
            vm((2, sides, HALO), f32),
            vm((2, sides, HALO), f32),
            vm((2, sides, HALO), f32),
            vm((nlev, 1, group), f32),
            vm((up8(3 * group), cells + 2 * FIELD_HALO + LANES), f32),
            vm((up8(3 * group) * ((cells + 2 * FIELD_HALO) // LANES + 2), 2 * LANES), bf16),
            vm((up8(3 * group) * ((cells + 2 * FIELD_HALO) // LANES + 2), 2 * LANES), bf16),
            vm((points, ext), i32),
            vm((points, ext), f32),
            vm((sides, ext), i32),
            vm((sides, ext), f32),
            vm((sides, ext), f32),
            vm((sides, ext), f32),
            vm((up8(3 * group), ext), f32),
            vm((nlev, group, ext), f32),
            vm((lrows, ext), f32),
            vm((lrows, ext), f32),
            vm((lrows, ext), f32),
            vm((lrows, ext), f32),
            pltpu.SemaphoreType.DMA((14,)),
            pltpu.SemaphoreType.DMA((14,)),
            pltpu.SemaphoreType.DMA((3, peers)),
            pltpu.SemaphoreType.DMA((3, peers)),
            pltpu.SemaphoreType.DMA((peers,)),
            pltpu.SemaphoreType.DMA((peers,)),
        ],
        compiler_params=pltpu.CompilerParams(
            collective_id=0, has_side_effects=True
        ),
    )(*args)
    return jnp.transpose(winds, (1, 0, 2)), height


def solution(mesh):
    in_specs = (
        P(None, "lev", "patch"),
        P(None, "lev", "patch"),
        P(None, "lev", "patch"),
        P(None, "patch"),
        P(None, "patch"),
        P(None, "patch"),
        P(None, "patch"),
        P(),
        P(),
        P("lev"),
    )
    out_specs = (P(None, "lev", "patch"), P("lev", "patch"))
    body = functools.partial(per_device, mesh.shape["patch"], mesh.shape["lev"])
    return jax.shard_map(
        body, mesh=mesh, in_specs=in_specs, out_specs=out_specs, check_vma=False
    )
```

time: 34.1 us -> 23.9 us (0.70)
  the two profiles are of different devices: /device:TPU:0 before, /device:TPU:1 now
where the time goes in v2:
time: 23.9 us; the launch traced here: 23.7 us
  Pallas kernels  20.7 us (87%)
  local copies, waits for them, and re-layouts  2.31 us (10%)
  between operations  0.65 us (3%)
    pallas_call x1, Pallas kernels, per_device(): pl.pallas_call(functools.partial(kernel, npatch, nlev), out_shape=(jax.Sh...  20.7 us
    unnamed x4, local copies, waits for them, and re-layouts  2.31 us

profile of v2, /device:TPU:1, one launch (start us, length us, event | category | flops | bytes accessed | tf_op | source)
XLA Modules:
  0.0 23.7 jit_solution(18106139897557485220)
XLA Ops:
  0.6 20.7 %shard_map.113 = (f32[12,2,2048]{2,1,0:T(2,128)}, f32[12,2048]{1,0:T(8,128)}) custom-call(f32[3,12,2048]{2,1,0:T(8,128)} %fields_in.1, s32[12,1,2048]{2,1,0:T(1,128)} %s_index_in.1, f32[12,1,2048]{2,1,0:T(1,128)} %s_weight_in.1, s32[6,2048]{1,0:T(8,128)} %nbr_in.1, f32[6,2048]{1,0:T(8,128)} %lap_in.1, f32[6,2048]{1,0:T(8,128)} %ex_in.1, f32[6,2048]{1,0:T(8,128)} %ey_in.1, ...), custom_call_target="tpu_custom_call" | custom-call | tf_op jit(solution)/shard_map/pallas_call | solution.py:459
  21.4 0.0 copy-start
  21.4 1.7 %copy.14 = f32[2,12,2048]{2,0,1:T(2,128)} copy(f32[2,12,2048]{2,0,1:T(2,128)} %bitcast.2) | data formatting | bytes 393216
  23.1 0.0 copy-done
  23.1 0.7 %copy.15 = f32[12,2048]{1,0:T(8,128)} copy(f32[12,2048]{1,0:T(8,128)S(1)} %copy-done) | data formatting | bytes 196608
Async XLA Ops:
  21.4 1.7 %copy-start = (f32[12,2048]{1,0:T(8,128)S(1)}, f32[12,2048]{1,0:T(8,128)}, u32[]{:S(2)}) copy-start(f32[12,2048]{1,0:T(8,128)} %get-tuple-element.9) | copy-start | bytes 294916

commit v3 on v2

--- a/solution.py
+++ b/solution.py
@@ -72,10 +72,10 @@
     npatch, nlev,
     fields_in, s_index_in, s_weight_in, nbr_in, lap_in, ex_in, ey_in, to_modes, from_modes, helm,
     winds_out, height_out,
-    fields, s_index, s_weight, nbr, lap, ex, ey, winds, load_sem, wind_sem,
+    fields, s_index, s_weight, nbr, lap, ex, ey, load_sem,
     f_halo, si_halo, sw_halo, nb_halo, lw_halo, ex_halo, ey_halo, hc,
     F, G0, G1, si, sw, nb, lw, gx, gy, U, rx, rinv, cinv, xa, xb,
-    send_sem, recv_sem, lev_send, lev_recv, hc_send, hc_recv,
+    near_sem, send_sem, recv_sem, lev_send, lev_recv, hc_send, hc_recv,
 ):
     group = fields.shape[1]
     cells = fields.shape[2]
@@ -92,8 +92,12 @@
     left = lax.rem(patch + npatch - 1, npatch)
 
     barrier = pltpu.get_barrier_semaphore()
-    for to in (left, right):
-        pl.semaphore_signal(barrier, inc=1, device_id={"patch": to}, device_id_type=MESH)
+    pl.semaphore_signal(barrier, inc=1, device_id={"patch": right}, device_id_type=MESH)
+
+    @pl.when(patch != 1)
+    def _():
+        pl.semaphore_signal(barrier, inc=1, device_id={"patch": left}, device_id_type=MESH)
+
     for d in range(1, nlev):
         pl.semaphore_signal(
             barrier, inc=1, device_id={"lev": lax.rem(lev + d, nlev)}, device_id_type=MESH
@@ -148,17 +152,21 @@
             for d in range(1, nlev)
         ]
 
-    def meet_and_send():
-        pl.semaphore_wait(barrier, 2 + nlev - 1)
-        for side in (0, 1):
-            for copy in halo_copies(side):
-                copy.start()
-        for copy in helm_copies():
+    def start(made):
+        for copy in made:
             copy.start()
 
     @pl.when(patch != 0)
     def _():
-        meet_and_send()
+        pl.semaphore_wait(barrier, 2 + nlev - 1)
+
+    @pl.when(patch == 1)
+    def _():
+        pl.semaphore_signal(near_sem, inc=1, device_id={"patch": left}, device_id_type=MESH)
+
+    @pl.when(patch != 0)
+    def _():
+        start(halo_copies(0) + halo_copies(1) + helm_copies())
 
     frows = F.shape[0]
     tiles = 2 * REACH // LANES + 1
@@ -316,7 +324,16 @@
         split_pair(tile, False, G0)
     for tile in range(own_lo + 1, own_hi, 2):
         split_pair(tile, True, G1)
-    for b in range(first, last):
+    middle = first + 2
+    for b in range(first, middle):
+        upstream(b, b % 2)
+
+    @pl.when(patch == 0)
+    def _():
+        pl.semaphore_wait(near_sem, 1)
+        start(halo_copies(0))
+
+    for b in range(middle, last):
         upstream(b, b % 2)
     nb[:, own] = nbr[...] + (HALO - NBR_REACH)
     lw[:, own] = lap[...]
@@ -325,12 +342,13 @@
 
     @pl.when(patch == 0)
     def _():
-        meet_and_send()
+        pl.semaphore_wait(barrier, 2 + nlev - 2)
+        start(halo_copies(1) + helm_copies())
 
     loop(*inner, right_side, inner[1])
     for copy in lev_copies(0, *inner):
         copy.start()
-    begin = jnp.where(patch == 1, 1, 1 - lax.rem(patch, 2))
+    begin = 1 - lax.rem(patch, 2)
 
     def flank(turn, carry):
         side = begin + turn * (1 - 2 * begin)
@@ -345,9 +363,7 @@
     lax.fori_loop(0, 2, flank, 0)
 
     for f in range(2):
-        winds[:, f, :] = U[f * group : (f + 1) * group, own]
-    winds_copy = pltpu.make_async_copy(winds, winds_out, wind_sem)
-    winds_copy.start()
+        winds_out[:, f, :] = U[f * group : (f + 1) * group, own]
 
     for copy in helm_copies():
         copy.wait()
@@ -435,7 +451,6 @@
     for copy in lev_copies(2, (1 - begin) * (last - 1), outer):
         copy.wait_recv()
     finish(1 - begin, False)
-    winds_copy.wait()
     for side in (0, 1):
         for copy in halo_copies(side):
             copy.wait_send()
@@ -446,6 +461,17 @@
             copy.wait_send()
 
 
+def hand_over(winds_in, height_in, winds_out, height_out, sem):
+    copies = [
+        pltpu.make_async_copy(winds_in, winds_out, sem.at[0]),
+        pltpu.make_async_copy(height_in, height_out, sem.at[1]),
+    ]
+    for copy in copies:
+        copy.start()
+    for copy in copies:
+        copy.wait()
+
+
 def per_device(npatch, nlev, *args):
     fields, s_index, _, nbr = args[:4]
     _, group, cells = fields.shape
@@ -453,26 +479,25 @@
     levels = group * nlev
     ext = cells + 2 * HALO
     args = args[:-1] + (args[-1].reshape(1, group),)
+    args = [pltpu.with_memory_space_constraint(a, pltpu.HBM) for a in args]
     lrows = up8(levels)
     vm = pltpu.VMEM
     peers = max(nlev - 1, 1)
     winds, height = pl.pallas_call(
         functools.partial(kernel, npatch, nlev),
         out_shape=(
-            jax.ShapeDtypeStruct((group, 2, cells), f32),
-            jax.ShapeDtypeStruct((group, cells), f32),
+            pltpu.VMEM((group, 2, cells), f32),
+            pltpu.VMEM((group, cells), f32),
         ),
         in_specs=[pl.BlockSpec(memory_space=pl.ANY)] * 7
         + [pl.BlockSpec(memory_space=pltpu.VMEM)] * 3,
         out_specs=(
-            pl.BlockSpec(memory_space=pl.ANY),
+            pl.BlockSpec(memory_space=pltpu.VMEM),
             pl.BlockSpec(memory_space=pltpu.VMEM),
         ),
         scratch_shapes=[vm(a.shape, a.dtype) for a in args[:7]]
         + [
-            vm((group, 2, cells), f32),
             pltpu.SemaphoreType.DMA((7,)),
-            pltpu.SemaphoreType.DMA,
             vm((2, 3, group, FIELD_HALO), f32),
             vm((2, points, 1, HALO), i32),
             vm((2, points, 1, HALO), f32),
@@ -496,6 +521,7 @@
             vm((lrows, ext), f32),
             vm((lrows, ext), f32),
             vm((lrows, ext), f32),
+            pltpu.SemaphoreType.REGULAR,
             pltpu.SemaphoreType.DMA((14,)),
             pltpu.SemaphoreType.DMA((14,)),
             pltpu.SemaphoreType.DMA((3, peers)),
@@ -504,9 +530,20 @@
             pltpu.SemaphoreType.DMA((peers,)),
         ],
         compiler_params=pltpu.CompilerParams(
-            collective_id=0, has_side_effects=True
+            collective_id=0, has_side_effects=True, vmem_limit_bytes=20 << 20
         ),
     )(*args)
+    winds, height = pl.pallas_call(
+        hand_over,
+        out_shape=(
+            jax.ShapeDtypeStruct(winds.shape, f32),
+            jax.ShapeDtypeStruct(height.shape, f32),
+        ),
+        in_specs=[pl.BlockSpec(memory_space=pltpu.VMEM)] * 2,
+        out_specs=(pl.BlockSpec(memory_space=pl.ANY),) * 2,
+        scratch_shapes=[pltpu.SemaphoreType.DMA((2,))],
+        compiler_params=pltpu.CompilerParams(vmem_limit_bytes=1 << 20),
+    )(winds, height)
     return jnp.transpose(winds, (1, 0, 2)), height
 
 

time: 23.9 us -> 20.4 us (0.85)
  the two profiles are of different devices: /device:TPU:1 before, /device:TPU:0 now
where the time goes in v3:
time: 20.4 us; the launch traced here: 20.2 us
  Pallas kernels  19.6 us (96%)
  between operations  0.64 us (3%)
    pallas_call x1, Pallas kernels, per_device(): pl.pallas_call(functools.partial(kernel, npatch, nlev), out_shape=(pltpu....  18.8 us
    pallas_call x1, Pallas kernels, per_device(): pl.pallas_call(hand_over, out_shape=(jax.ShapeDtypeStruct(winds.shape, f3...  0.74 us

profile of v3, /device:TPU:0, one launch (start us, length us, event | category | flops | bytes accessed | tf_op | source)
XLA Modules:
  0.0 20.2 jit_solution(12950047739684732453)
XLA Ops:
  0.6 18.8 %shard_map.113 = (f32[12,2,2048]{2,1,0:T(2,128)S(1)}, f32[12,2048]{1,0:T(8,128)S(1)}) custom-call(f32[3,12,2048]{2,1,0:T(8,128)} %fields_in.1, s32[12,1,2048]{2,1,0:T(1,128)} %s_index_in.1, f32[12,1,2048]{2,1,0:T(1,128)} %s_weight_in.1, s32[6,2048]{1,0:T(8,128)} %nbr_in.1, f32[6,2048]{1,0:T(8,128)} %lap_in.1, f32[6,2048]{1,0:T(8,128)} %ex_in.1, ...), custom_call_target="tpu_custom_call" | custom-call | tf_op jit(solution)/shard_map/pallas_call | solution.py:486
  19.5 0.7 %shard_map.114 = (f32[12,2,2048]{2,1,0:T(2,128)}, f32[12,2048]{1,0:T(8,128)}) custom-call(f32[12,2,2048]{2,1,0:T(2,128)S(1)} %get-tuple-element.6.winds_in, f32[12,2048]{1,0:T(8,128)S(1)} %get-tuple-element.7.height_in), custom_call_target="tpu_custom_call" | custom-call | tf_op jit(solution)/shard_map/pallas_call | solution.py:536

commit v4 on v3

--- a/solution.py
+++ b/solution.py
@@ -74,7 +74,7 @@
     winds_out, height_out,
     fields, s_index, s_weight, nbr, lap, ex, ey, load_sem,
     f_halo, si_halo, sw_halo, nb_halo, lw_halo, ex_halo, ey_halo, hc,
-    F, G0, G1, si, sw, nb, lw, gx, gy, U, rx, rinv, cinv, xa, xb,
+    F, G, si, sw, nb, lw, gx, gy, U, rx, rinv, cinv, xa, xb,
     near_sem, send_sem, recv_sem, lev_send, lev_recv, hc_send, hc_recv,
 ):
     group = fields.shape[1]
@@ -174,29 +174,29 @@
     own_lo = FIELD_HALO // LANES
     own_hi = own_lo + own_blocks
 
-    def split_pair(tile, odd, to):
-        start = tile * frows + (frows if odd else 0) % (2 * SUB)
-        if not isinstance(tile, int):
+    def tile_rows(tile, count, odd):
+        start = tile * frows + odd * (G.shape[0] // 2 + frows % (2 * SUB))
+        if not isinstance(start, int):
             start = pl.multiple_of(start, 2 * SUB)
-        rows = pl.ds(start, 2 * frows)
+        return pl.ds(start, count * frows)
+
+    def split_pair(tile, odd):
+        rows = tile_rows(tile, 2, odd)
         high, low = split(
             jnp.concatenate([F[:, cols_of(tile)], F[:, cols_of(tile + 1)]], axis=0)
         )
-        to[rows, 0:LANES] = high
-        to[rows, LANES : 2 * LANES] = low
+        G[rows, 0:LANES] = high
+        G[rows, LANES : 2 * LANES] = low
 
     lane_id = lax.broadcasted_iota(i32, (LANES, LANES), 0).astype(f32).astype(bf16)
     one = jnp.ones((LANES, LANES), bf16)
     zero = jnp.zeros((LANES, LANES), bf16)
 
-    def upstream(b, odd, by_lane=(2, 5)):
+    def upstream(b, odd, t0=0, count=tiles, by_lane=(2, 5), add=False):
         cols = cols_of(b)
         nv = frows // SUB
         acc = [None] * nv
-        start = b * frows + (frows if odd else 0) % (2 * SUB)
-        if not isinstance(b, int):
-            start = pl.multiple_of(start, 2 * SUB)
-        field = (G1 if odd else G0).at[pl.ds(start, tiles * frows), :]
+        field = G.at[tile_rows(b + t0, count, odd), :]
         for pair_no in range(points // 2):
             pair = (2 * pair_no, 2 * pair_no + 1)
             his, los = [], []
@@ -206,31 +206,25 @@
                 los.append(x & (LANES - 1))
             on_lanes = pair_no in by_lane
             if not on_lanes:
-                hot = []
-                for lo in los:
-                    lo = jnp.broadcast_to(lo[0:1].astype(f32), (LANES, LANES))
-                    h = jnp.where(lane_id == lo.astype(bf16), one, zero)
-                    hot.append(jnp.concatenate([h, h], axis=0))
-                got = jnp.dot(
-                    field[...], jnp.concatenate(hot, axis=1), preferred_element_type=f32
-                )
+                got = jnp.dot(field[...], one_hot(los), preferred_element_type=f32)
             for no, q in enumerate(pair):
                 w = row8(sw, q, cols)
-                here = [his[no] == t for t in range(tiles)]
+                here = [his[no] - t0 == t for t in range(count)]
                 for r in range(nv):
-                    sel = None
-                    for t in range(tiles):
+                    sel = None if count == tiles else jnp.zeros((SUB, LANES), f32)
+                    for t in range(count):
                         row = t * frows + r * SUB
                         if on_lanes:
                             taken = lanes_of(
-                                F[r * SUB : (r + 1) * SUB, cols_of(b + t)], los[no]
+                                F[r * SUB : (r + 1) * SUB, cols_of(b + t0 + t)], los[no]
                             )
                         else:
                             taken = got[row : row + SUB, no * LANES : (no + 1) * LANES]
                         sel = taken if sel is None else jnp.where(here[t], taken, sel)
                     acc[r] = w * sel if acc[r] is None else acc[r] + w * sel
         for r in range(nv):
-            U[r * SUB : (r + 1) * SUB, cols] = acc[r]
+            at = slice(r * SUB, (r + 1) * SUB)
+            U[at, cols] = U[at, cols] + acc[r] if add else acc[r]
 
     lane = lax.broadcasted_iota(i32, (SUB, LANES), 1)
     low_half = lane < NBR_REACH
@@ -251,6 +245,36 @@
         x = row8(nb, k, cols)
         return x & (LANES - 1), (x >> BITS) == b
 
+    def one_hot(los):
+        hot = []
+        for lo in los:
+            lo = jnp.broadcast_to(lo[0:1].astype(f32), (LANES, LANES))
+            h = jnp.where(lane_id == lo.astype(bf16), one, zero)
+            hot.append(jnp.concatenate([h, h], axis=0))
+        return jnp.concatenate(hot, axis=1)
+
+    def beside(own_t, far_t, b, cols):
+        nv = len(own_t)
+        places = [place(k, b, cols) for k in range(sides)]
+        by_product = range(sides - 2, sides)
+        if len(by_product):
+            high, low = split(jnp.concatenate(own_t + far_t, axis=0))
+            got = jnp.dot(
+                jnp.concatenate([high, low], axis=1),
+                one_hot([places[k][0] for k in by_product]),
+                preferred_element_type=f32,
+            )
+        for k in range(sides):
+            lo, here = places[k]
+            for r in range(nv):
+                if k in by_product:
+                    at = (k - by_product[0]) * LANES
+                    mine = got[r * SUB : (r + 1) * SUB, at : at + LANES]
+                    far = got[(nv + r) * SUB : (nv + r + 1) * SUB, at : at + LANES]
+                else:
+                    mine, far = lanes_of(own_t[r], lo), lanes_of(far_t[r], lo)
+                yield k, r, jnp.where(here, mine, far)
+
     wrows = up8(2 * group)
     sub_iota = lax.broadcasted_iota(i32, (SUB, LANES), 0)
 
@@ -259,18 +283,15 @@
         nv = wrows // SUB
         own_t, far_t = around(U, b, nv)
         acc = [jnp.zeros((SUB, LANES), f32)] * nv
-        for k in range(sides):
-            lo, here = place(k, b, cols)
+        for k, r, taken in beside(own_t, far_t, b, cols):
             wx, wy = row8(gx, k, cols), row8(gy, k, cols)
-            for r in range(nv):
-                if (r + 1) * SUB <= group:
-                    w = wx
-                elif r * SUB >= group:
-                    w = wy
-                else:
-                    w = jnp.where(sub_iota + r * SUB < group, wx, wy)
-                taken = jnp.where(here, lanes_of(own_t[r], lo), lanes_of(far_t[r], lo))
-                acc[r] = acc[r] + w * (taken - own_t[r])
+            if (r + 1) * SUB <= group:
+                w = wx
+            elif r * SUB >= group:
+                w = wy
+            else:
+                w = jnp.where(sub_iota + r * SUB < group, wx, wy)
+            acc[r] = acc[r] + w * (taken - own_t[r])
         both = jnp.concatenate(acc, axis=0)
         div = both[0:group] + both[group : 2 * group]
         rx[lev, :, cols] = U[2 * group : 3 * group, cols] - COUPLING * div
@@ -301,9 +322,9 @@
         for f in range(3):
             F[f * group : (f + 1) * group, at] = f_halo[side, f]
         for i in range(0, own_lo, 2):
-            split_pair(side * own_hi + i, False, G0)
+            split_pair(side * own_hi + i, 0)
         for i in range(1, own_lo + 2, 2):
-            split_pair(side * (own_hi - 2) + i, True, G1)
+            split_pair(side * (own_hi - 2) + i, 1)
         at = pl.ds(pl.multiple_of(side * (HALO + cells), LANES), HALO)
         shift = HALO + (2 * side - 1) * cells
         si[:, at] = si_halo[side, :, 0, :] + shift
@@ -321,9 +342,9 @@
     si[:, own] = s_index[:, 0, :] + HALO
     sw[:, own] = s_weight[:, 0, :]
     for tile in range(own_lo, own_hi, 2):
-        split_pair(tile, False, G0)
+        split_pair(tile, 0)
     for tile in range(own_lo + 1, own_hi, 2):
-        split_pair(tile, True, G1)
+        split_pair(tile, 1)
     middle = first + 2
     for b in range(first, middle):
         upstream(b, b % 2)
@@ -350,17 +371,31 @@
         copy.start()
     begin = 1 - lax.rem(patch, 2)
 
-    def flank(turn, carry):
-        side = begin + turn * (1 - 2 * begin)
+    def flank(side, turn):
         arrive(side)
-        for i in range(first):
-            upstream(side * last + i, i % 2)
+        if turn == 0:
+            for i in range(first):
+                upstream(side * last + i, i % 2)
+        else:
+            for i in range(hb):
+                upstream(side * (nb_blocks - hb) + i, i % 2, by_lane=())
+            for m in range(mixed):
+                upstream(near(side, m), 0, side * (tiles - 1 - m), m + 1, range(points), True)
         loop(side * (last - 1), outer, right_side, outer)
         for copy in lev_copies(1 + turn, side * (last - 1), outer):
             copy.start()
-        return carry
-
-    lax.fori_loop(0, 2, flank, 0)
+
+    mixed = first - hb
+
+    def near(side, m):
+        return first - 1 - m + side * (last - first + 1 + 2 * m)
+
+    flank(begin, 0)
+    side = 1 - begin
+    for m in range(mixed):
+        b, t0 = near(side, m), (1 - side) * (m + 1)
+        upstream(b, lax.rem(b + t0, 2), t0, tiles - 1 - m)
+    flank(side, 1)
 
     for f in range(2):
         winds_out[:, f, :] = U[f * group : (f + 1) * group, own]
@@ -406,12 +441,9 @@
         cols = cols_of(b)
         own_t, far_t = around(x_old, b, nv)
         acc = [None] * nv
-        for k in range(sides):
-            lo, here = place(k, b, cols)
-            w = row8(lw, k, cols)
-            for r in range(nv):
-                term = w * jnp.where(here, lanes_of(own_t[r], lo), lanes_of(far_t[r], lo))
-                acc[r] = term if acc[r] is None else acc[r] + term
+        for k, r, taken in beside(own_t, far_t, b, cols):
+            term = row8(lw, k, cols) * taken
+            acc[r] = term if acc[r] is None else acc[r] + term
         for r in range(nv):
             rows = pl.ds(r * SUB, SUB)
             s = steps[j][r * SUB : (r + 1) * SUB]
@@ -507,8 +539,7 @@
             vm((2, sides, HALO), f32),
             vm((nlev, 1, group), f32),
             vm((up8(3 * group), cells + 2 * FIELD_HALO + LANES), f32),
-            vm((up8(3 * group) * ((cells + 2 * FIELD_HALO) // LANES + 2), 2 * LANES), bf16),
-            vm((up8(3 * group) * ((cells + 2 * FIELD_HALO) // LANES + 2), 2 * LANES), bf16),
+            vm((2 * up8(3 * group) * ((cells + 2 * FIELD_HALO) // LANES + 2), 2 * LANES), bf16),
             vm((points, ext), i32),
             vm((points, ext), f32),
             vm((sides, ext), i32),

time: 20.4 us -> 19.7 us (0.966)
  Pallas kernels: 19.6 us -> 18.9 us
    pallas_call x1, Pallas kernels: 18.8 us -> 18.1 us  [per_device(): pl.pallas_call(functools.partial(kernel, npatch, nlev), out_shape=(pltpu....]
where the time goes in v4:
time: 19.7 us; the launch traced here: 19.5 us
  Pallas kernels  18.9 us (96%)
  between operations  0.64 us (3%)
    pallas_call x1, Pallas kernels, per_device(): pl.pallas_call(functools.partial(kernel, npatch, nlev), out_shape=(pltpu....  18.1 us
    pallas_call x1, Pallas kernels, per_device(): pl.pallas_call(hand_over, out_shape=(jax.ShapeDtypeStruct(winds.shape, f3...  0.74 us

profile of v4, /device:TPU:0, one launch (start us, length us, event | category | flops | bytes accessed | tf_op | source)
XLA Modules:
  0.0 19.5 jit_solution(12105373310351434994)
XLA Ops:
  0.6 18.1 %shard_map.113 = (f32[12,2,2048]{2,1,0:T(2,128)S(1)}, f32[12,2048]{1,0:T(8,128)S(1)}) custom-call(f32[3,12,2048]{2,1,0:T(8,128)} %fields_in.1, s32[12,1,2048]{2,1,0:T(1,128)} %s_index_in.1, f32[12,1,2048]{2,1,0:T(1,128)} %s_weight_in.1, s32[6,2048]{1,0:T(8,128)} %nbr_in.1, f32[6,2048]{1,0:T(8,128)} %lap_in.1, f32[6,2048]{1,0:T(8,128)} %ex_in.1, ...), custom_call_target="tpu_custom_call" | custom-call | tf_op jit(solution)/shard_map/pallas_call | solution.py:518
  18.8 0.7 %shard_map.114 = (f32[12,2,2048]{2,1,0:T(2,128)}, f32[12,2048]{1,0:T(8,128)}) custom-call(f32[12,2,2048]{2,1,0:T(2,128)S(1)} %get-tuple-element.6.winds_in, f32[12,2048]{1,0:T(8,128)S(1)} %get-tuple-element.7.height_in), custom_call_target="tpu_custom_call" | custom-call | tf_op jit(solution)/shard_map/pallas_call | solution.py:567

commit v5 on v4

--- a/solution.py
+++ b/solution.py
@@ -74,7 +74,7 @@
     winds_out, height_out,
     fields, s_index, s_weight, nbr, lap, ex, ey, load_sem,
     f_halo, si_halo, sw_halo, nb_halo, lw_halo, ex_halo, ey_halo, hc,
-    F, G, si, sw, nb, lw, gx, gy, U, rx, rinv, cinv, xa, xb,
+    F, G, L, si, sw, nb, lw, gx, gy, U, rx, rinv, cinv, xa, xb, xs0, xs1,
     near_sem, send_sem, recv_sem, lev_send, lev_recv, hc_send, hc_recv,
 ):
     group = fields.shape[1]
@@ -245,6 +245,31 @@
         x = row8(nb, k, cols)
         return x & (LANES - 1), (x >> BITS) == b
 
+    window_id = lax.broadcasted_iota(i32, (2 * LANES, LANES), 0).astype(f32).astype(bf16)
+
+    def wide(x):
+        return jnp.broadcast_to(x[0:1], (2 * LANES, LANES)).astype(bf16)
+
+    def neighbour_matrix(b):
+        cols = cols_of(b)
+        at, weight = [], []
+        for q in range(sides):
+            lo, here = place(q, b, cols)
+            at.append(jnp.where(here, lo, lo + LANES))
+            weight.append(row8(lw, q, cols))
+        for q in range(sides):
+            for p in range(q + 1, sides):
+                weight[q] = weight[q] + jnp.where(at[q] == at[p], row8(lw, p, cols), 0.0)
+        high = jnp.zeros((2 * LANES, LANES), bf16)
+        low = jnp.zeros((2 * LANES, LANES), bf16)
+        for q in reversed(range(sides)):
+            w_high = weight[q].astype(bf16).astype(f32)
+            hit = window_id == wide(at[q].astype(f32))
+            high = jnp.where(hit, wide(w_high), high)
+            low = jnp.where(hit, wide(weight[q] - w_high), low)
+        L[b, :, 0:LANES] = high
+        L[b, :, LANES : 2 * LANES] = low
+
     def one_hot(los):
         hot = []
         for lo in los:
@@ -345,9 +370,14 @@
         split_pair(tile, 0)
     for tile in range(own_lo + 1, own_hi, 2):
         split_pair(tile, 1)
+    nb[:, own] = nbr[...] + (HALO - NBR_REACH)
+    lw[:, own] = lap[...]
+    gx[:, own] = ex[...]
+    gy[:, own] = ey[...]
     middle = first + 2
     for b in range(first, middle):
         upstream(b, b % 2)
+        neighbour_matrix(b)
 
     @pl.when(patch == 0)
     def _():
@@ -356,10 +386,7 @@
 
     for b in range(middle, last):
         upstream(b, b % 2)
-    nb[:, own] = nbr[...] + (HALO - NBR_REACH)
-    lw[:, own] = lap[...]
-    gx[:, own] = ex[...]
-    gy[:, own] = ey[...]
+        neighbour_matrix(b)
 
     @pl.when(patch == 0)
     def _():
@@ -376,9 +403,11 @@
         if turn == 0:
             for i in range(first):
                 upstream(side * last + i, i % 2)
+                neighbour_matrix(side * last + i)
         else:
             for i in range(hb):
                 upstream(side * (nb_blocks - hb) + i, i % 2, by_lane=())
+                neighbour_matrix(side * (nb_blocks - hb) + i)
             for m in range(mixed):
                 upstream(near(side, m), 0, side * (tiles - 1 - m), m + 1, range(points), True)
         loop(side * (last - 1), outer, right_side, outer)
@@ -395,6 +424,7 @@
     for m in range(mixed):
         b, t0 = near(side, m), (1 - side) * (m + 1)
         upstream(b, lax.rem(b + t0, 2), t0, tiles - 1 - m)
+        neighbour_matrix(b)
     flank(side, 1)
 
     for f in range(2):
@@ -426,6 +456,7 @@
     def modal(b):
         cols = cols_of(b)
         wsum = jnp.sum(lw[:, cols], axis=0, keepdims=True)
+        new = []
         total = product(to_parts, jnp.concatenate([rx[g, :, cols] for g in range(nlev)], axis=0))
         for r in range(nv):
             rows = pl.ds(r * SUB, SUB)
@@ -434,22 +465,36 @@
             scaled = total[r * SUB : (r + 1) * SUB] * inv
             rinv[rows, cols] = scaled
             cinv[rows, cols] = cr * inv
-            xa[rows, cols] = steps[0][r * SUB : (r + 1) * SUB] * scaled
+            new.append(steps[0][r * SUB : (r + 1) * SUB] * scaled)
+            xa[rows, cols] = new[r]
+        xs0[:, cols] = stack(jnp.concatenate(new, axis=0))
+
+    def stack(x):
+        return jnp.concatenate([x, x - x.astype(bf16).astype(f32)], axis=0).astype(bf16)
 
     def sweep(j, b):
         x_old, x_new = (xa, xb) if j % 2 else (xb, xa)
         cols = cols_of(b)
-        own_t, far_t = around(x_old, b, nv)
-        acc = [None] * nv
-        for k, r, taken in beside(own_t, far_t, b, cols):
-            term = row8(lw, k, cols) * taken
-            acc[r] = term if acc[r] is None else acc[r] + term
+        s_old, s_new = (xs0, xs1) if j % 2 else (xs1, xs0)
+        around_b = jnp.where(
+            wide_low, s_old[:, cols_of(jnp.minimum(b + 1, nb_blocks - 1))], s_old[:, cols_of(jnp.maximum(b - 1, 0))]
+        )
+        got = jnp.dot(
+            jnp.concatenate([s_old[:, cols], around_b], axis=1), L[b], preferred_element_type=f32
+        )
+        acc = (got[0:lrows, 0:LANES] + got[0:lrows, LANES:]) + (got[lrows:, 0:LANES] + got[lrows:, LANES:])
+        new = []
         for r in range(nv):
             rows = pl.ds(r * SUB, SUB)
             s = steps[j][r * SUB : (r + 1) * SUB]
-            x_new[rows, cols] = (1.0 - s) * own_t[r] + s * (
-                rinv[rows, cols] + cinv[rows, cols] * acc[r]
-            )
+            new.append((1.0 - s) * x_old[rows, cols] + s * (
+                rinv[rows, cols] + cinv[rows, cols] * acc[r * SUB : (r + 1) * SUB]
+            ))
+            x_new[rows, cols] = new[r]
+        if j < SWEEPS - 1:
+            s_new[:, cols] = stack(jnp.concatenate(new, axis=0))
+
+    wide_low = lax.broadcasted_iota(i32, (2 * lrows, LANES), 1).astype(f32).astype(bf16) < NBR_REACH
 
     x_end = xa if SWEEPS % 2 else xb
 
@@ -540,6 +585,7 @@
             vm((nlev, 1, group), f32),
             vm((up8(3 * group), cells + 2 * FIELD_HALO + LANES), f32),
             vm((2 * up8(3 * group) * ((cells + 2 * FIELD_HALO) // LANES + 2), 2 * LANES), bf16),
+            vm((ext // LANES, 2 * LANES, 2 * LANES), bf16),
             vm((points, ext), i32),
             vm((points, ext), f32),
             vm((sides, ext), i32),
@@ -552,6 +598,8 @@
             vm((lrows, ext), f32),
             vm((lrows, ext), f32),
             vm((lrows, ext), f32),
+            vm((2 * lrows, ext), bf16),
+            vm((2 * lrows, ext), bf16),
             pltpu.SemaphoreType.REGULAR,
             pltpu.SemaphoreType.DMA((14,)),
             pltpu.SemaphoreType.DMA((14,)),

time: 19.7 us -> 19 us (0.964)
  Pallas kernels: 18.9 us -> 18.1 us
    pallas_call x1, Pallas kernels: 18.1 us -> 17.4 us  [per_device(): pl.pallas_call(functools.partial(kernel, npatch, nlev), out_shape=(pltpu....]
where the time goes in v5:
time: 19 us; the launch traced here: 18.8 us
  Pallas kernels  18.1 us (95%)
  between operations  0.64 us (3%)
    pallas_call x1, Pallas kernels, per_device(): pl.pallas_call(functools.partial(kernel, npatch, nlev), out_shape=(pltpu....  17.4 us
    pallas_call x1, Pallas kernels, per_device(): pl.pallas_call(hand_over, out_shape=(jax.ShapeDtypeStruct(winds.shape, f3...  0.74 us

profile of v5, /device:TPU:0, one launch (start us, length us, event | category | flops | bytes accessed | tf_op | source)
XLA Modules:
  0.0 18.8 jit_solution(8645044353221427792)
XLA Ops:
  0.6 17.4 %shard_map.113 = (f32[12,2,2048]{2,1,0:T(2,128)S(1)}, f32[12,2048]{1,0:T(8,128)S(1)}) custom-call(f32[3,12,2048]{2,1,0:T(8,128)} %fields_in.1, s32[12,1,2048]{2,1,0:T(1,128)} %s_index_in.1, f32[12,1,2048]{2,1,0:T(1,128)} %s_weight_in.1, s32[6,2048]{1,0:T(8,128)} %nbr_in.1, f32[6,2048]{1,0:T(8,128)} %lap_in.1, f32[6,2048]{1,0:T(8,128)} %ex_in.1, ...), custom_call_target="tpu_custom_call" | custom-call | tf_op jit(solution)/shard_map/pallas_call | solution.py:563
  18.0 0.7 %shard_map.114 = (f32[12,2,2048]{2,1,0:T(2,128)}, f32[12,2048]{1,0:T(8,128)}) custom-call(f32[12,2,2048]{2,1,0:T(2,128)S(1)} %get-tuple-element.6.winds_in, f32[12,2048]{1,0:T(8,128)S(1)} %get-tuple-element.7.height_in), custom_call_target="tpu_custom_call" | custom-call | tf_op jit(solution)/shard_map/pallas_call | solution.py:615

commit v6 on v5

--- a/solution.py
+++ b/solution.py
@@ -122,9 +122,10 @@
         (lap_in, lw_halo, HALO),
     )
 
-    def halo_copies(side):
+    def halo_copies(side, kinds=range(7)):
         made = []
-        for no, (src, dst, width) in enumerate(pairs):
+        for no in kinds:
+            src, dst, width = pairs[no]
             lead = (slice(None),) * (len(src.shape) - 1)
             start = (1 - side) * (cells - width)
             if not isinstance(side, int):
@@ -341,7 +342,7 @@
         ]
 
     def arrive(side):
-        for copy in halo_copies(side):
+        for copy in halo_copies(side, range(3)):
             copy.wait_recv()
         at = pl.ds(pl.multiple_of(side * (FIELD_HALO + cells), LANES), FIELD_HALO)
         for f in range(3):
@@ -354,6 +355,12 @@
         shift = HALO + (2 * side - 1) * cells
         si[:, at] = si_halo[side, :, 0, :] + shift
         sw[:, at] = sw_halo[side, :, 0, :]
+
+    def arrive_grid(side):
+        for copy in halo_copies(side, range(3, 7)):
+            copy.wait_recv()
+        at = pl.ds(pl.multiple_of(side * (HALO + cells), LANES), HALO)
+        shift = HALO + (2 * side - 1) * cells
         nb[:, at] = nb_halo[side] + (shift - NBR_REACH)
         lw[:, at] = lw_halo[side]
         gx[:, at] = ex_halo[side]
@@ -401,18 +408,22 @@
     def flank(side, turn):
         arrive(side)
         if turn == 0:
+            arrive_grid(side)
             for i in range(first):
                 upstream(side * last + i, i % 2)
-                neighbour_matrix(side * last + i)
+                if i < first - 1:
+                    neighbour_matrix(side * (last - 1) + 1 + i)
         else:
             for i in range(hb):
                 upstream(side * (nb_blocks - hb) + i, i % 2, by_lane=())
-                neighbour_matrix(side * (nb_blocks - hb) + i)
             for m in range(mixed):
                 upstream(near(side, m), 0, side * (tiles - 1 - m), m + 1, range(points), True)
+            arrive_grid(side)
         loop(side * (last - 1), outer, right_side, outer)
         for copy in lev_copies(1 + turn, side * (last - 1), outer):
             copy.start()
+        if turn:
+            neighbour_matrix(side * (nb_blocks - 3) + 1)
 
     mixed = first - hb
 

time: 19 us -> 18.6 us (0.979)
  Pallas kernels: 18.1 us -> 17.7 us
    pallas_call x1, Pallas kernels: 17.4 us -> 16.9 us  [per_device(): pl.pallas_call(functools.partial(kernel, npatch, nlev), out_shape=(pltpu....]
where the time goes in v6:
time: 18.6 us; the launch traced here: 18.3 us
  Pallas kernels  17.7 us (95%)
  between operations  0.64 us (3%)
    pallas_call x1, Pallas kernels, per_device(): pl.pallas_call(functools.partial(kernel, npatch, nlev), out_shape=(pltpu....  16.9 us
    pallas_call x1, Pallas kernels, per_device(): pl.pallas_call(hand_over, out_shape=(jax.ShapeDtypeStruct(winds.shape, f3...  0.74 us

profile of v6, /device:TPU:0, one launch (start us, length us, event | category | flops | bytes accessed | tf_op | source)
XLA Modules:
  0.0 18.3 jit_solution(15712278741498955208)
XLA Ops:
  0.6 16.9 %shard_map.113 = (f32[12,2,2048]{2,1,0:T(2,128)S(1)}, f32[12,2048]{1,0:T(8,128)S(1)}) custom-call(f32[3,12,2048]{2,1,0:T(8,128)} %fields_in.1, s32[12,1,2048]{2,1,0:T(1,128)} %s_index_in.1, f32[12,1,2048]{2,1,0:T(1,128)} %s_weight_in.1, s32[6,2048]{1,0:T(8,128)} %nbr_in.1, f32[6,2048]{1,0:T(8,128)} %lap_in.1, f32[6,2048]{1,0:T(8,128)} %ex_in.1, ...), custom_call_target="tpu_custom_call" | custom-call | tf_op jit(solution)/shard_map/pallas_call | solution.py:574
  17.6 0.7 %shard_map.114 = (f32[12,2,2048]{2,1,0:T(2,128)}, f32[12,2048]{1,0:T(8,128)}) custom-call(f32[12,2,2048]{2,1,0:T(2,128)S(1)} %get-tuple-element.6.winds_in, f32[12,2048]{1,0:T(8,128)S(1)} %get-tuple-element.7.height_in), custom_call_target="tpu_custom_call" | custom-call | tf_op jit(solution)/shard_map/pallas_call | solution.py:626

commit v7 on v6

--- a/solution.py
+++ b/solution.py
@@ -403,6 +403,8 @@
     loop(*inner, right_side, inner[1])
     for copy in lev_copies(0, *inner):
         copy.start()
+    early = (outer + 1) // 2
+    pieces = (((1, 0, outer),), ((2, 0, early), (3, early, outer - early)))
     begin = 1 - lax.rem(patch, 2)
 
     def flank(side, turn):
@@ -419,9 +421,11 @@
             for m in range(mixed):
                 upstream(near(side, m), 0, side * (tiles - 1 - m), m + 1, range(points), True)
             arrive_grid(side)
-        loop(side * (last - 1), outer, right_side, outer)
-        for copy in lev_copies(1 + turn, side * (last - 1), outer):
-            copy.start()
+        at = side * (last - 1)
+        for no, skip, count in pieces[turn]:
+            loop(at + skip, count, right_side, count)
+            for copy in lev_copies(no, at + skip, count):
+                copy.start()
         if turn:
             neighbour_matrix(side * (nb_blocks - 3) + 1)
 
@@ -536,16 +540,17 @@
     for copy in lev_copies(0, *inner) + lev_copies(1, begin * (last - 1), outer):
         copy.wait_recv()
     finish(begin, True)
-    for copy in lev_copies(2, (1 - begin) * (last - 1), outer):
-        copy.wait_recv()
+    for no, skip, count in pieces[1]:
+        for copy in lev_copies(no, (1 - begin) * (last - 1) + skip, count):
+            copy.wait_recv()
     finish(1 - begin, False)
     for side in (0, 1):
         for copy in halo_copies(side):
             copy.wait_send()
     for copy in lev_copies(0, *inner):
         copy.wait_send()
-    for no in (1, 2):
-        for copy in lev_copies(no, 0, outer):
+    for no, skip, count in pieces[0] + pieces[1]:
+        for copy in lev_copies(no, skip, count):
             copy.wait_send()
 
 
@@ -614,8 +619,8 @@
             pltpu.SemaphoreType.REGULAR,
             pltpu.SemaphoreType.DMA((14,)),
             pltpu.SemaphoreType.DMA((14,)),
-            pltpu.SemaphoreType.DMA((3, peers)),
-            pltpu.SemaphoreType.DMA((3, peers)),
+            pltpu.SemaphoreType.DMA((4, peers)),
+            pltpu.SemaphoreType.DMA((4, peers)),
             pltpu.SemaphoreType.DMA((peers,)),
             pltpu.SemaphoreType.DMA((peers,)),
         ],

time: 18.6 us -> 18.5 us (level)
  no operation moved by 1% of the time
where the time goes in v7:
time: 18.5 us; the launch traced here: 18.2 us
  Pallas kernels  17.6 us (95%)
  between operations  0.64 us (3%)
    pallas_call x1, Pallas kernels, per_device(): pl.pallas_call(functools.partial(kernel, npatch, nlev), out_shape=(pltpu....  16.8 us
    pallas_call x1, Pallas kernels, per_device(): pl.pallas_call(hand_over, out_shape=(jax.ShapeDtypeStruct(winds.shape, f3...  0.74 us

profile of v7, /device:TPU:0, one launch (start us, length us, event | category | flops | bytes accessed | tf_op | source)
XLA Modules:
  0.0 18.2 jit_solution(15411909269582790297)
XLA Ops:
  0.6 16.8 %shard_map.113 = (f32[12,2,2048]{2,1,0:T(2,128)S(1)}, f32[12,2048]{1,0:T(8,128)S(1)}) custom-call(f32[3,12,2048]{2,1,0:T(8,128)} %fields_in.1, s32[12,1,2048]{2,1,0:T(1,128)} %s_index_in.1, f32[12,1,2048]{2,1,0:T(1,128)} %s_weight_in.1, s32[6,2048]{1,0:T(8,128)} %nbr_in.1, f32[6,2048]{1,0:T(8,128)} %lap_in.1, f32[6,2048]{1,0:T(8,128)} %ex_in.1, ...), custom_call_target="tpu_custom_call" | custom-call | tf_op jit(solution)/shard_map/pallas_call | solution.py:579
  17.5 0.7 %shard_map.114 = (f32[12,2,2048]{2,1,0:T(2,128)}, f32[12,2048]{1,0:T(8,128)}) custom-call(f32[12,2,2048]{2,1,0:T(2,128)S(1)} %get-tuple-element.6.winds_in, f32[12,2048]{1,0:T(8,128)S(1)} %get-tuple-element.7.height_in), custom_call_target="tpu_custom_call" | custom-call | tf_op jit(solution)/shard_map/pallas_call | solution.py:631
